TPU v7x, 512 devices: a whole 4x8x8 slice. The times are simulated.
512 devices in a mesh: seq: 8 (over z), mp: 16 (over y, core), dp: 4 (over x).
Axes of the slice: x: 4, y: 8, z: 8, core: 2. Of those that a mesh axis runs over, the one named last changes fastest.
Arguments:
- tokens: bfloat16 [65536, 2048], P(('dp', 'seq'), 'mp'), parts along dimension 0, may hold values from -6 to 6
- w_query: bfloat16 [2048, 2048], P(None, 'mp'), may hold values from -0.125 to 0.125
- w_key: bfloat16 [2048, 2048], P(None, 'mp'), may hold values from -0.125 to 0.125
- w_value: bfloat16 [2048, 2048], P(None, 'mp'), may hold values from -0.125 to 0.125
- w_gate: bfloat16 [2048, 2048], P(None, 'mp'), may hold values from -0.125 to 0.125
- decay_exponent: int32 [16], P('mp'), may hold values from 5 to 16
- forget: float32 [65536, 16], P(('dp', 'seq'), 'mp'), parts along dimension 0, may hold values from 0 to 0.69
- norm_gain: float32 [2048], replicated, may hold values from 0.1 to 1.9
Outputs:
- retained: bfloat16 [65536, 2048], P(('dp', 'seq', 'mp')), parts along dimension 0
There are 4 independent parts, one for each index of `dp`. A program takes and returns all parts, laid end to end along the dimension named above; an argument that names none is the same for every part. Nothing has to cross between parts.
All inputs are finite; a program needn't handle non-finite values.
Results may differ from a plain program's by a relative error of at most 0.015.
Values may be sent and summed in bfloat16 or wider, within the bound.
A program may use at most 64 MiB of HBM per device.

v0:
```python
import jax
import jax.numpy as jnp
from jax import lax
from jax.sharding import PartitionSpec as P

HEADS = 16
DH = 128


def from_everyone(shard, axis):
    copies = jnp.broadcast_to(shard, (lax.axis_size(axis), *shard.shape))
    return lax.all_to_all(copies, axis, split_axis=0, concat_axis=0, tiled=True)


def collected_together(shard, axis):
    leaves = jax.tree.leaves(shard)
    sequence = sorted(range(len(leaves)), key=lambda k: -leaves[k].size)
    width = (1, *leaves[sequence[0]].shape)[-1]
    lines = [
        jnp.pad(leaves[k].reshape(-1), (0, -leaves[k].size % width)).reshape(-1, width)
        for k in sequence
    ]
    both, at, found = (from_everyone(jnp.concatenate(lines), axis), 0, {})
    for k, line in zip(sequence, lines):
        section = both[:, at : at + len(line)].reshape(len(both), -1)
        found[k] = section[:, : leaves[k].size].reshape(-1, *leaves[k].shape)
        at += len(line)
    numbers = iter(range(len(leaves)))
    return jax.tree.map(lambda _: found[next(numbers)], shard)


def folded_in_pairs(pieces, combine):
    while len(jax.tree.leaves(pieces)[0]) > 1:
        pieces = jax.vmap(combine)(
            *(jax.tree.map(lambda part: part[side::2], pieces) for side in (0, 1))
        )
    return jax.tree.map(lambda part: part[0], pieces)


def prefix_2(shard, axis, combine, identity):
    size, index = (lax.axis_size(axis), lax.axis_index(axis))
    passed = jnp.arange(size) < index

    def kept(part, zero, own):
        part = jnp.where(
            passed.reshape(-1, *(1 for _ in own.shape)),
            part.astype(own.dtype),
            jnp.asarray(zero, own.dtype),
        )
        return part

    pieces = collected_together(
        jax.tree.map(lambda part, kind: part.astype(kind), shard, (jnp.bfloat16, jnp.bfloat16)),
        axis,
    )
    return folded_in_pairs(jax.tree.map(kept, pieces, identity, shard), combine)


def over_copies(shard, axis):
    return from_everyone(shard, axis).sum(axis=0)


def run_blocks(queries, key_rows, values, logdecay, head_count, head_width):
    seq_rows = queries.shape[0]
    block_rows = 512
    block_count = seq_rows // block_rows

    def shaped(source):
        return source.reshape(block_count, block_rows, head_count, head_width)

    decays = logdecay.reshape(block_count, block_rows, head_count)
    position = lax.broadcasted_iota(jnp.int32, (block_rows, block_rows), 0)
    earlier = lax.broadcasted_iota(jnp.int32, (block_rows, block_rows), 1)
    causal = position >= earlier

    def advance(carried, pieces):
        kv_state, offset = carried
        query_blk, key_blk, value_blk, decay_blk = pieces
        running = jnp.cumsum(decay_blk, axis=0)
        heads_first = running.T
        log_gap = heads_first[:, :, None] - heads_first[:, None, :]
        decay_mask = jnp.where(causal[None], jnp.exp(jnp.where(causal[None], log_gap, 0.0)), 0.0)
        scores = jnp.einsum("tha,sha->hts", query_blk, key_blk, preferred_element_type=jnp.float32)
        scores = (scores * decay_mask).astype(jnp.bfloat16)
        inner = jnp.einsum("hts,shb->thb", scores, value_blk, preferred_element_type=jnp.float32)
        query_float = query_blk.astype(jnp.float32)
        earlier_part = jnp.einsum(
            "tha,hab->thb", query_float * jnp.exp(running)[:, :, None], kv_state
        )
        query_device = query_float * jnp.exp(running + offset[None, :])[:, :, None]
        key_scaled = key_blk.astype(jnp.float32) * jnp.exp(running[-1:] - running)[:, :, None]
        kv_state = jnp.exp(running[-1])[:, None, None] * kv_state + jnp.einsum(
            "sha,shb->hab", key_scaled, value_blk.astype(jnp.float32)
        )
        return ((kv_state, offset + running[-1]), (inner + earlier_part, query_device))

    initial = (
        jnp.zeros((head_count, head_width, head_width), jnp.float32),
        jnp.zeros((head_count,), jnp.float32),
    )
    final, outputs = lax.scan(
        advance, initial, (shaped(queries), shaped(key_rows), shaped(values), decays)
    )
    local_part = outputs[0].reshape(seq_rows, head_count, head_width)
    query_device = outputs[1].reshape(seq_rows, head_count, head_width)
    return (local_part, query_device, final[0], final[1])


def combine_states(before, after):
    return (before[0] * after[0], after[0][:, None, None] * before[1] + after[1])


def body(tokens, w_query, w_key, w_value, w_gate, decay_exponent, forget, norm_gain):
    seq_rows = tokens.shape[0]
    local_width = w_query.shape[1]
    head_count = decay_exponent.shape[0]
    head_width = local_width // head_count
    empty = jnp.zeros((seq_rows, local_width), jnp.float32)
    summed = (empty, empty, empty, empty)
    piece = lax.all_gather(tokens, "mp", axis=1, tiled=True)
    results = []
    for weight, partial_value in zip((w_query, w_key, w_value, w_gate), summed):
        results.append(jnp.dot(piece, weight, preferred_element_type=jnp.float32))
    projected = tuple(results)
    queries = projected[0].astype(jnp.bfloat16)
    key_rows = (projected[1] * DH ** (-0.5)).astype(jnp.bfloat16)
    values = projected[2].astype(jnp.bfloat16)
    gate = projected[3].astype(jnp.bfloat16)
    rate = jnp.log1p(-jnp.exp2(-decay_exponent.astype(jnp.float32)))
    logdecay = rate[None, :] - forget
    local_part, query_device, own_state, own_total = run_blocks(
        queries, key_rows, values, logdecay, head_count, head_width
    )
    prefix = prefix_2(
        (jnp.exp(own_total), own_state),
        "seq",
        combine_states,
        (jnp.ones_like(own_total), jnp.zeros_like(own_state)),
    )
    incoming = prefix[1]
    from_before = jnp.einsum("tha,hab->thb", query_device, incoming)
    output = (local_part + from_before).astype(jnp.bfloat16).reshape(seq_rows, local_width)
    output_float = output.astype(jnp.float32)
    squares = over_copies(jnp.sum(output_float * output_float, axis=1), "mp")
    rstd = lax.rsqrt(squares / (HEADS * DH) + 1e-06)
    gain_here = lax.dynamic_slice_in_dim(
        norm_gain, lax.axis_index("mp") * local_width, local_width, 0
    )
    gated = (
        jax.nn.silu(gate.astype(jnp.float32)) * output_float * rstd[:, None] * gain_here[None, :]
    )
    return lax.all_to_all(gated.astype(jnp.bfloat16), "mp", split_axis=0, concat_axis=1, tiled=True)


def solution(mesh):
    placed = (
        P(("dp", "seq"), "mp"),
        P(None, "mp"),
        P(None, "mp"),
        P(None, "mp"),
        P(None, "mp"),
        P("mp"),
        P(("dp", "seq"), "mp"),
        P(),
    )
    return jax.shard_map(
        body, mesh=mesh, in_specs=placed, out_specs=P(("dp", "seq", "mp"), None), check_vma=False
    )
```

profile of v0, /device:TPU:1, one launch (start us, length us, event | category | flops | bytes accessed | tf_op | source)
XLA Modules:
  0.0 194.3 jit_solution(12837014939397995423)
XLA Ops:
  8.7 76.1 %all-gather.2.cloned.1.call-done = bf16[2048,2048]{1,0:T(8,128)(2,1)} async-done(((bf16[2048,128]{1,0:T(8,128)(2,1)}), bf16[2048,2048]{1,0:T(8,128)(2,1)}) %all-gather.2.cloned.1.call-update) | async-done | bytes 8388624 | tf_op jit(solution)/shard_map/all_gather | solution.py:120
  84.8 5.9 %fusion.52 = bf16[2048,128]{1,0:T(8,128)(2,1)S(1)} fusion(bf16[2048,2048]{1,0:T(8,128)(2,1)} %all-gather.2.cloned.1.call-done, bf16[2048,128]{1,0:T(8,128)(2,1)S(1)} %copy-done), kind=kOutput, calls=%fused_computation.61 | convolution fusion | flops 1074266112 | bytes 9437184 | tf_op jit(solution)/shard_map/dot_general | solution.py:123
  90.7 3.3 %convolution_convert_fusion.1 = bf16[2048,128]{1,0:T(8,128)(2,1)} fusion(bf16[2048,2048]{1,0:T(8,128)(2,1)S(1)} %copy-done.1, bf16[2048,128]{1,0:T(8,128)(2,1)S(1)} %copy-done.2), kind=kOutput, calls=%fused_computation.57 | convolution fusion | flops 1074003968 | bytes 9437184 | tf_op jit(solution)/shard_map/dot_general | solution.py:123
  94.0 2.4 %convolution_convert_fusion = bf16[2048,128]{1,0:T(8,128)(2,1)S(1)} fusion(bf16[2048,2048]{1,0:T(8,128)(2,1)S(1)} %copy-done.1, bf16[2048,128]{1,0:T(8,128)(2,1)S(1)} %copy-done.3), kind=kOutput, calls=%fused_computation.56 | convolution fusion | flops 1074003968 | bytes 9437184 | tf_op jit(solution)/shard_map/dot_general | solution.py:123
  96.4 29.3 %while.18 = (s32[]{:T(128)}, f32[1,128,128]{2,1,0:T(8,128)S(1)}, f32[1]{0:T(128)}, f32[4,512,1,128]{3,1,0,2:T(8,128)S(1)}, bf16[4,512,1,128]{3,1,2,0:T(8,128)(2,...) while((s32[]{:T(128)}, f32[1,128,128]{2,1,0:T(8,128)S(1)}, ...), condition=%wide.region_3.4_spmd.clone.clone, body=%wide.region_0.3_spmd.clone.clone.sunk | while | flops 169935888 | bytes 3247952 | solution.py:101
  99.9 1.5 fusion.91
  101.6 1.3 fusion.90
  102.9 0.8 fusion.92
  107.3 1.5 fusion.91
  108.9 1.3 fusion.90
  110.2 0.8 fusion.92
  114.6 1.5 fusion.91
  116.2 1.3 fusion.90
  117.5 0.8 fusion.92
  121.9 1.5 fusion.91
  123.5 1.3 fusion.90
  126.5 4.0 %all-to-all-start = ((bf16[8,129,128]{2,1,0:T(8,128)(2,1)}), bf16[8,129,128]{2,1,0:T(8,128)(2,1)S(1)}, u32[]{:S(2)}, u32[]{:S(2)}) async-start(bf16[8,129,128]{2,1,0:T(8,128)(2,1)} %broadcast_in_dim.45), calls=%async_computation | async-start | bytes 557056 | tf_op jit(solution)/shard_map/all_to_all | solution.py:12
  130.5 12.5 %all-to-all-done = bf16[8,129,128]{2,1,0:T(8,128)(2,1)S(1)} async-done(((bf16[8,129,128]{2,1,0:T(8,128)(2,1)}), bf16[8,129,128]{2,1,0:T(8,128)(2,1)S(1)}, u32[]{:S(2)}, u32[]{:S(2)}) %all-to-all-start) | async-done | bytes 264224 | tf_op jit(solution)/shard_map/all_to_all | solution.py:12
  144.2 2.1 %multiply_reduce_fusion = (f32[2048]{0:T(1024)S(1)}, f32[2048,128]{1,0:T(8,128)S(1)}) fusion(f32[2048,1,128]{2,0,1:T(8,128)S(1)} %bitcast.167, bf16[2048,128]{1,0:T(8,128)(2,1)} %bitcast.171, f32[2,1,128,128]{3,2,1,0:T(8,128)S(1)} %slice_add_fusion.1, f32[]{:T(128)} %bitcast.12), kind=kOutput, calls=%fused_computation.65 | convolution fusion | flops 68450304 | bytes 2760708 | tf_op jit(solution)/shard_map/tha,hab->thb/dot_general | solution.py:141
  147.0 4.9 %all-to-all-start.1 = ((f32[16,1,2048]{2,1,0:T(1,128)}), f32[16,1,2048]{2,1,0:T(1,128)S(1)}, u32[]{:S(2)}, u32[]{:S(2)}) async-start(f32[16,1,2048]{2,1,0:T(1,128)} %broadcast_in_dim.49), calls=%async_computation.1 | async-start | bytes 262144 | tf_op jit(solution)/shard_map/all_to_all | solution.py:12
  152.7 8.1 %all-to-all-done.1 = f32[16,1,2048]{2,1,0:T(1,128)S(1)} async-done(((f32[16,1,2048]{2,1,0:T(1,128)}), f32[16,1,2048]{2,1,0:T(1,128)S(1)}, u32[]{:S(2)}, u32[]{:S(2)}) %all-to-all-start.1) | async-done | bytes 131104 | tf_op jit(solution)/shard_map/all_to_all | solution.py:12
  160.9 5.8 %multiply_convert_fusion = bf16[2048,128]{1,0:T(8,128)(2,1)S(1)} fusion(f32[2048,128]{1,0:T(8,128)S(1)} %get-tuple-element.204, bf16[2048,2048]{1,0:T(8,128)(2,1)} %all-gather.2.cloned.1.call-done, bf16[2048,128]{1,0:T(8,128)(2,1)} %param.14, f32[128]{0:T(128)S(1)} %dynamic_slice.17, f32[2048]{0:T(1024)S(1)} %add_rsqrt_fusion), kind=kOutput, calls=%fused_computation.64 | convolution fusion | flops 1076363264 | bytes 10494464 | tf_op jit(solution)/shard_map/dot_general | solution.py:123
  166.7 19.9 %all_to_all.30 = bf16[16,128,128]{2,1,0:T(8,128)(2,1)S(1)} all-to-all(bf16[16,128,128]{2,1,0:T(8,128)(2,1)S(1)} %bitcast.170), channel_id=1, replica_groups=mesh['seq'=8,'mp'=16,'dp'=4] {'mp'}, dimensions={0} | all-to-all | bytes 1048576 | tf_op jit(solution)/shard_map/all_to_all | solution.py:152
  186.6 0.9 copy_bitcast_fusion
  (89 shorter events, 15.7 us)
Async XLA Ops:
  6.5 78.2 %copy-start = (bf16[2048,128]{1,0:T(8,128)(2,1)S(1)}, bf16[2048,128]{1,0:T(8,128)(2,1)}, u32[]{:S(2)}) copy-start(bf16[2048,128]{1,0:T(8,128)(2,1)} %param.12) | copy-start | bytes 1572868
  6.5 84.1 %copy-start.2 = (bf16[2048,128]{1,0:T(8,128)(2,1)S(1)}, bf16[2048,128]{1,0:T(8,128)(2,1)}, u32[]{:S(2)}) copy-start(bf16[2048,128]{1,0:T(8,128)(2,1)} %param.13) | copy-start | bytes 1572868
  6.5 78.2 %all-gather.2.cloned.1.call-start = ((), (), s32[]{:S(2)}) async-start(), calls=%async_computation.3 | async-start | bytes 8912896 | tf_op jit(solution)/shard_map/all_gather | solution.py:120
  84.8 5.9 %copy-start.1 = (bf16[2048,2048]{1,0:T(8,128)(2,1)S(1)}, bf16[2048,2048]{1,0:T(8,128)(2,1)}, u32[]{:S(2)}) copy-start(bf16[2048,2048]{1,0:T(8,128)(2,1)} %all-gather.2.cloned.1.call-done) | copy-start | bytes 25165828
  90.7 3.3 %copy-start.3 = (bf16[2048,128]{1,0:T(8,128)(2,1)S(1)}, bf16[2048,128]{1,0:T(8,128)(2,1)}, u32[]{:S(2)}) copy-start(bf16[2048,128]{1,0:T(8,128)(2,1)} %param.11) | copy-start | bytes 1572868
  126.5 16.6 %all-to-all-start = ((bf16[8,129,128]{2,1,0:T(8,128)(2,1)}), bf16[8,129,128]{2,1,0:T(8,128)(2,1)S(1)}, u32[]{:S(2)}, u32[]{:S(2)}) async-start(bf16[8,129,128]{2,1,0:T(8,128)(2,1)} %broadcast_in_dim.45), calls=%async_computation | async-start | bytes 557056 | tf_op jit(solution)/shard_map/all_to_all | solution.py:12
  147.0 13.8 %all-to-all-start.1 = ((f32[16,1,2048]{2,1,0:T(1,128)}), f32[16,1,2048]{2,1,0:T(1,128)S(1)}, u32[]{:S(2)}, u32[]{:S(2)}) async-start(f32[16,1,2048]{2,1,0:T(1,128)} %broadcast_in_dim.49), calls=%async_computation.1 | async-start | bytes 262144 | tf_op jit(solution)/shard_map/all_to_all | solution.py:12
Sparse Core Ops, SparseCore 0:
  9.4 75.3 all-gather.1
where the time goes:
time: 195 us; the launch traced here: 194 us
  waiting for transfers between devices  97.4 us (50%)
  matrix products  31.5 us (16%)
  blocking collectives  19.9 us (10%)
  between operations  14.3 us (7%)
  local copies, waits for them, and re-layouts  10.2 us (5%)
  starting transfers between devices  8.92 us (5%)
  other arithmetic  6.83 us (4%)
  loops' own time  5.24 us (3%)
    all_gather x1, waiting for transfers between devices, body(): piece = lax.all_gather(tokens, 'mp', axis=1, tiled=True)  76.1 us
    all_to_all x2, waiting for transfers between devices, from_everyone(): return lax.all_to_all(copies, axis, split_axis=0, concat_axis=0, tiled=True)  20.7 us
    all_to_all x1, blocking collectives, body(): lax.all_to_all(gated.astype(jnp.bfloat16), 'mp', split_axis=0, concat_axi...  19.9 us
    dot_general x4, matrix products, body(): results.append(jnp.dot(piece, weight, preferred_element_type=jnp.float32))  17.3 us
    all_to_all x2, starting transfers between devices, from_everyone(): return lax.all_to_all(copies, axis, split_axis=0, concat_axis=0, tiled=True)  8.92 us
    dot_general x4, matrix products, advance(): jnp.einsum('hts,shb->thb', scores, value_blk, preferred_element_type=jnp....  5.87 us
    another operation x1, loops' own time, run_blocks(): lax.scan(advance, initial, (shaped(queries), shaped(key_rows), shaped(val...  5.24 us
    dot_general x4, matrix products, advance(): jnp.einsum('sha,shb->hab', key_scaled, value_blk.astype(jnp.float32))  5.01 us
  transfers between devices with their start and end apart: 3, of which 3 were waited for; matrix products, arithmetic and copies ran while one was open for 1% of the time, Pallas kernels for 0%

commit v1 on v0

--- a/solution.py
+++ b/solution.py
@@ -2,6 +2,7 @@
 import jax.numpy as jnp
 from jax import lax
 from jax.sharding import PartitionSpec as P
+from jax.lax import all_to_all, axis_size
 
 HEADS = 16
 DH = 128
@@ -117,7 +118,10 @@
     head_width = local_width // head_count
     empty = jnp.zeros((seq_rows, local_width), jnp.float32)
     summed = (empty, empty, empty, empty)
-    piece = lax.all_gather(tokens, "mp", axis=1, tiled=True)
+    bank = []
+    for _ in range(axis_size("mp")):
+        bank.append(tokens)
+    piece = jnp.concatenate(all_to_all(jnp.stack(bank, 0), "mp", 0, 0), 1)
     results = []
     for weight, partial_value in zip((w_query, w_key, w_value, w_gate), summed):
         results.append(jnp.dot(piece, weight, preferred_element_type=jnp.float32))

time: 195 us -> 315 us (1.62)
  waiting for transfers between devices: 97.4 us -> 201 us
  starting transfers between devices: 8.92 us -> 26.4 us
  between operations: 14.3 us -> 0.99 us
  matrix products: 31.5 us -> 38.4 us
  local copies, waits for them, and re-layouts: 10.2 us -> 16 us
    all_to_all x0 -> x1, waiting for transfers between devices: none -> 183 us  [body(): piece = jnp.concatenate(all_to_all(jnp.stack(bank, 0), 'mp', 0, 0), 1)]
    all_gather x1 -> x0, waiting for transfers between devices: 76.1 us -> none  [body(): piece = lax.all_gather(tokens, 'mp', axis=1, tiled=True)]
    all_to_all x0 -> x1, starting transfers between devices: none -> 11.4 us  [body(): piece = jnp.concatenate(all_to_all(jnp.stack(bank, 0), 'mp', 0, 0), 1)]
    dot_general x4, matrix products: 17.3 us -> 24.3 us  [body(): results.append(jnp.dot(piece, weight, preferred_element_type=jnp.float32))]
    all_to_all x2, starting transfers between devices: 8.92 us -> 14.9 us  [from_everyone(): return lax.all_to_all(copies, axis, split_axis=0, concat_axis=0, tiled=True)]
    another operation x8 -> x9, local copies, waits for them, and re-layouts: 0.3 us -> 4.6 us  [the longest x1 4.3 us: body(): piece = jnp.concatenate(all_to_all(jnp.stack(bank, 0), 'mp', 0, 0), 1)]
  transfers between devices with their start and end apart: 3 -> 3, of which waited for: 3 -> 3; matrix products, arithmetic and copies ran while one was open for 1% -> 0% of each run, Pallas kernels for 0% -> 0%
where the time goes in v1:
time: 315 us
  waiting for transfers between devices  201 us (64%)
  matrix products  38.4 us (12%)
  starting transfers between devices  26.4 us (8%)
  blocking collectives  19.9 us (6%)
  local copies, waits for them, and re-layouts  16 us (5%)
  other arithmetic  6.13 us (2%)
  loops' own time  5.47 us (2%)
    all_to_all x1, waiting for transfers between devices, body(): piece = jnp.concatenate(all_to_all(jnp.stack(bank, 0), 'mp', 0, 0), 1)  183 us
    dot_general x4, matrix products, body(): results.append(jnp.dot(piece, weight, preferred_element_type=jnp.float32))  24.3 us
    all_to_all x1, blocking collectives, body(): lax.all_to_all(gated.astype(jnp.bfloat16), 'mp', split_axis=0, concat_axi...  19.9 us
    all_to_all x2, waiting for transfers between devices, from_everyone(): return lax.all_to_all(copies, axis, split_axis=0, concat_axis=0, tiled=True)  18.7 us
    all_to_all x2, starting transfers between devices, from_everyone(): return lax.all_to_all(copies, axis, split_axis=0, concat_axis=0, tiled=True)  14.9 us
    all_to_all x1, starting transfers between devices, body(): piece = jnp.concatenate(all_to_all(jnp.stack(bank, 0), 'mp', 0, 0), 1)  11.4 us
  transfers between devices with their start and end apart: 3, of which 3 were waited for; matrix products, arithmetic and copies ran while one was open for 0% of the time, Pallas kernels for 0%

profile of v1, /device:TPU:1, one launch (start us, length us, event | category | flops | bytes accessed | tf_op | source)
XLA Modules:
  0.0 314.6 jit_solution(14915818654427561245)
XLA Ops:
  0.0 1.3 copy.56
  1.3 4.3 %stack.2 = bf16[16,2048,128]{1,2,0:T(8,128)(2,1)} broadcast(bf16[2048,128]{0,1:T(8,128)(2,1)S(1)} %copy.56), dimensions={1,2} | broadcast | bytes 8912896 | tf_op jit(solution)/shard_map/stack | solution.py:124
  5.6 11.4 %all-to-all-start = ((bf16[16,2048,128]{1,2,0:T(8,128)(2,1)}), bf16[16,2048,128]{1,2,0:T(8,128)(2,1)}, u32[]{:S(2)}, u32[]{:S(2)}) async-start(bf16[16,2048,128]{1,2,0:T(8,128)(2,1)} %stack.2), calls=%async_computation | async-start | bytes 16777216 | tf_op jit(solution)/shard_map/all_to_all | solution.py:124
  17.9 182.6 %all-to-all-done = bf16[16,2048,128]{1,2,0:T(8,128)(2,1)} async-done(((bf16[16,2048,128]{1,2,0:T(8,128)(2,1)}), bf16[16,2048,128]{1,2,0:T(8,128)(2,1)}, u32[]{:S(2)}, u32[]{:S(2)}) %all-to-all-start) | async-done | bytes 8388640 | tf_op jit(solution)/shard_map/all_to_all | solution.py:124
  200.5 5.8 %convolution_convert_fusion = bf16[2048,128]{1,0:T(8,128)(2,1)S(1)} fusion(bf16[2048,2048]{0,1:T(8,128)(2,1)} %bitcast.1, bf16[2048,128]{1,0:T(8,128)(2,1)S(1)} %copy-done), kind=kOutput, calls=%fused_computation.56 | convolution fusion | flops 1074003968 | bytes 9437184 | tf_op jit(solution)/shard_map/dot_general | solution.py:127
  206.3 5.8 %fusion.52 = bf16[2048,128]{1,0:T(8,128)(2,1)S(1)} fusion(bf16[2048,2048]{0,1:T(8,128)(2,1)} %bitcast.1, bf16[2048,128]{1,0:T(8,128)(2,1)S(1)} %copy-done.2), kind=kOutput, calls=%fused_computation.61 | convolution fusion | flops 1074266112 | bytes 9437184 | tf_op jit(solution)/shard_map/dot_general | solution.py:127
  212.2 6.6 %convolution_convert_fusion.1 = bf16[2048,128]{1,0:T(8,128)(2,1)} fusion(bf16[2048,2048]{0,1:T(8,128)(2,1)} %bitcast.1, bf16[2048,128]{1,0:T(8,128)(2,1)S(1)} %copy-done.3), kind=kOutput, calls=%fused_computation.57 | convolution fusion | flops 1074003968 | bytes 9437184 | tf_op jit(solution)/shard_map/dot_general | solution.py:127
  218.8 29.6 %while.18 = (s32[]{:T(128)}, f32[1,128,128]{2,1,0:T(8,128)S(1)}, f32[1]{0:T(128)}, f32[4,512,1,128]{3,1,0,2:T(8,128)S(1)}, bf16[4,512,1,128]{3,1,2,0:T(8,128)(2,...) while((s32[]{:T(128)}, f32[1,128,128]{2,1,0:T(8,128)S(1)}, ...), condition=%wide.region_3.4_spmd.clone.clone, body=%wide.region_0.3_spmd.clone.clone.sunk | while | flops 169935888 | bytes 3247952 | solution.py:102
  222.5 1.5 fusion.91
  224.2 1.3 fusion.90
  229.9 1.5 fusion.91
  231.6 1.3 fusion.90
  237.3 1.5 fusion.91
  239.0 1.3 fusion.90
  244.7 1.5 fusion.91
  246.4 1.3 fusion.90
  249.3 7.3 %all-to-all-start.1 = ((bf16[8,129,128]{2,1,0:T(8,128)(2,1)}), bf16[8,129,128]{2,1,0:T(8,128)(2,1)S(1)}, u32[]{:S(2)}, u32[]{:S(2)}) async-start(bf16[8,129,128]{2,1,0:T(8,128)(2,1)} %broadcast_in_dim.45), calls=%async_computation.1 | async-start | bytes 557056 | tf_op jit(solution)/shard_map/all_to_all | solution.py:13
  256.6 10.6 %all-to-all-done.1 = bf16[8,129,128]{2,1,0:T(8,128)(2,1)S(1)} async-done(((bf16[8,129,128]{2,1,0:T(8,128)(2,1)}), bf16[8,129,128]{2,1,0:T(8,128)(2,1)S(1)}, u32[]{:S(2)}, u32[]{:S(2)}) %all-to-all-start.1) | async-done | bytes 264224 | tf_op jit(solution)/shard_map/all_to_all | solution.py:13
  268.3 2.1 multiply_reduce_fusion
  271.1 7.7 %all-to-all-start.2 = ((f32[16,1,2048]{2,1,0:T(1,128)}), f32[16,1,2048]{2,1,0:T(1,128)S(1)}, u32[]{:S(2)}, u32[]{:S(2)}) async-start(f32[16,1,2048]{2,1,0:T(1,128)} %broadcast_in_dim.49), calls=%async_computation.2 | async-start | bytes 262144 | tf_op jit(solution)/shard_map/all_to_all | solution.py:13
  279.6 8.1 %all-to-all-done.2 = f32[16,1,2048]{2,1,0:T(1,128)S(1)} async-done(((f32[16,1,2048]{2,1,0:T(1,128)}), f32[16,1,2048]{2,1,0:T(1,128)S(1)}, u32[]{:S(2)}, u32[]{:S(2)}) %all-to-all-start.2) | async-done | bytes 131104 | tf_op jit(solution)/shard_map/all_to_all | solution.py:13
  287.8 6.0 %multiply_convert_fusion = bf16[2048,128]{1,0:T(8,128)(2,1)S(1)} fusion(f32[2048,128]{1,0:T(8,128)S(1)} %get-tuple-element.204, bf16[2048,2048]{0,1:T(8,128)(2,1)} %bitcast.1, bf16[2048,128]{1,0:T(8,128)(2,1)} %param.14, f32[128]{0:T(128)S(1)} %dynamic_slice.17, f32[2048]{0:T(1024)S(1)} %add_rsqrt_fusion), kind=kOutput, calls=%fused_computation.64 | convolution fusion | flops 1076363264 | bytes 10494464 | tf_op jit(solution)/shard_map/dot_general | solution.py:127
  293.8 19.9 %all_to_all.35 = bf16[16,128,128]{2,1,0:T(8,128)(2,1)S(1)} all-to-all(bf16[16,128,128]{2,1,0:T(8,128)(2,1)S(1)} %bitcast.173), channel_id=1, replica_groups=mesh['seq'=8,'mp'=16,'dp'=4] {'mp'}, dimensions={0} | all-to-all | bytes 1048576 | tf_op jit(solution)/shard_map/all_to_all | solution.py:156
  313.7 0.9 copy_bitcast_fusion
  (90 shorter events, 16.8 us)
Async XLA Ops:
  0.0 200.5 %copy-start = (bf16[2048,128]{1,0:T(8,128)(2,1)S(1)}, bf16[2048,128]{1,0:T(8,128)(2,1)}, u32[]{:S(2)}) copy-start(bf16[2048,128]{1,0:T(8,128)(2,1)} %param.11) | copy-start | bytes 1572868
  5.6 12.3 %copy-start.1 = (f32[2048,1]{0,1:T(1,128)S(1)}, f32[2048,1]{0,1:T(1,128)}, u32[]{:S(2)}) copy-start(f32[2048,1]{0,1:T(1,128)} %param.16) | copy-start | bytes 24580
  5.6 194.9 %all-to-all-start = ((bf16[16,2048,128]{1,2,0:T(8,128)(2,1)}), bf16[16,2048,128]{1,2,0:T(8,128)(2,1)}, u32[]{:S(2)}, u32[]{:S(2)}) async-start(bf16[16,2048,128]{1,2,0:T(8,128)(2,1)} %stack.2), calls=%async_computation | async-start | bytes 16777216 | tf_op jit(solution)/shard_map/all_to_all | solution.py:124
  17.1 189.2 %copy-start.2 = (bf16[2048,128]{1,0:T(8,128)(2,1)S(1)}, bf16[2048,128]{1,0:T(8,128)(2,1)}, u32[]{:S(2)}) copy-start(bf16[2048,128]{1,0:T(8,128)(2,1)} %param.12) | copy-start | bytes 1572868
  206.3 5.9 %copy-start.3 = (bf16[2048,128]{1,0:T(8,128)(2,1)S(1)}, bf16[2048,128]{1,0:T(8,128)(2,1)}, u32[]{:S(2)}) copy-start(bf16[2048,128]{1,0:T(8,128)(2,1)} %param.13) | copy-start | bytes 1572868
  249.3 17.9 %all-to-all-start.1 = ((bf16[8,129,128]{2,1,0:T(8,128)(2,1)}), bf16[8,129,128]{2,1,0:T(8,128)(2,1)S(1)}, u32[]{:S(2)}, u32[]{:S(2)}) async-start(bf16[8,129,128]{2,1,0:T(8,128)(2,1)} %broadcast_in_dim.45), calls=%async_computation.1 | async-start | bytes 557056 | tf_op jit(solution)/shard_map/all_to_all | solution.py:13
  271.1 16.5 %all-to-all-start.2 = ((f32[16,1,2048]{2,1,0:T(1,128)}), f32[16,1,2048]{2,1,0:T(1,128)S(1)}, u32[]{:S(2)}, u32[]{:S(2)}) async-start(f32[16,1,2048]{2,1,0:T(1,128)} %broadcast_in_dim.49), calls=%async_computation.2 | async-start | bytes 262144 | tf_op jit(solution)/shard_map/all_to_all | solution.py:13
